TPU v7x, 32 devices: a whole 2x2x4 slice. The times are simulated.
32 devices in a mesh: station: 16 (over z, x, core), chan: 2 (over y).
Axes of the slice: x: 2, y: 2, z: 4, core: 2. Of those that a mesh axis runs over, the one named last changes fastest.
Arguments:
- samples: float32 [2, 16, 256, 128, 256], P(None, 'station', 'chan'), may hold values from -6 to 6
- weights: float32 [2, 16, 32, 256, 256], P(None, 'station', None, 'chan'), may hold values from -6 to 6
- antenna_flags: int32 [16, 256], P('station', 'chan'), may hold values from 0 to 1, as said below
- subband_table: int32 [256], replicated, may hold values from 0 to 255, each once
Outputs:
- visibilities: float32 [256, 2, 16, 32, 16], P('chan', None, 'station')
Inputs may be any that keep to these rules, and one draw needn't show every extreme that they name: `antenna_flags`: every station has at least 32 antennas with flag 1. `subband_table`: a permutation of 0 to 255.
All inputs are finite; a program needn't handle non-finite values.
Results may differ from a plain program's by a relative error of at most 0.0019.
Values may be sent and summed in bfloat16 or wider, within the bound.
A program may use at most 192 MiB of HBM per device.

v0:
```python
import functools

import jax
import jax.numpy as jnp
from jax import lax
from jax.experimental import pallas as pl
from jax.experimental.pallas import tpu as pltpu
from jax.sharding import PartitionSpec as P

LANES = 128
ANTENNAS_PER_STEP = 32
UNROLL = 8
STATIONS_PER_STEP = 4


def split(value):
    high = value.astype(jnp.bfloat16)
    low = (value - high.astype(jnp.float32)).astype(jnp.bfloat16)
    return high, low


def beam_kernel(table_ref, x_ref, w_ref, usable_ref, sent_ref, own_ref, slot_ref, x_rows, w_rows, *, antennas, beams):
    block, step = pl.program_id(0), pl.program_id(1)
    mine = lax.axis_index("chan")
    subbands = sent_ref.shape[0]
    kept = own_ref.shape[0] - 1
    x_stride = x_rows.shape[0] // LANES
    w_stride = w_rows.shape[0] // LANES
    x_step = x_ref.shape[2]
    w_step = w_ref.shape[2]

    @pl.when((block == 0) & (step == 0))
    def _():
        @pl.loop(0, subbands)
        def _(slot):
            slot_ref[table_ref[slot]] = slot

    for part in range(2):
        for a in range(x_step):
            row = part * antennas + step * x_step + a
            x_rows[pl.ds(row, LANES, stride=x_stride), :] = x_ref[part, 0, a].T
        for b in range(w_step):
            tile = w_ref[part, 0, b]
            if antennas < LANES:
                tile = jnp.concatenate([tile, jnp.zeros((LANES - antennas, LANES), jnp.float32)], axis=0)
            row = part * beams + step * w_step + b
            w_rows[pl.ds(row, LANES, stride=w_stride), :] = tile.T

    @pl.when(step == pl.num_programs(1) - 1)
    def _():
        usable = usable_ref[...]

        def one(f):
            x = x_rows[pl.ds(pl.multiple_of(f * x_stride, 8), 2 * antennas), :]
            w = w_rows[pl.ds(pl.multiple_of(f * w_stride, 8), 2 * beams), :][:, :antennas] * usable
            w_re, w_im = w[:beams], w[beams:]
            steer = jnp.concatenate(
                [jnp.concatenate([w_re, -w_im], axis=1), jnp.concatenate([w_im, w_re], axis=1)], axis=0
            )
            x_pair = jnp.concatenate(split(x), axis=1)
            w_pair = jnp.concatenate(split(steer), axis=0)
            grid = jnp.dot(w_pair, x_pair, preferred_element_type=jnp.float32)
            rows, cols = 2 * beams, x.shape[1]
            total = grid[:rows, :cols] + (grid[rows:, :cols] + grid[:rows, cols:] + grid[rows:, cols:])
            slot = slot_ref[block * LANES + f]
            sent_ref[slot] = total.astype(jnp.bfloat16)
            local = slot - mine * kept
            own_ref[jnp.where((local >= 0) & (local < kept), local, kept)] = total

        @pl.loop(0, LANES // UNROLL)
        def _(group):
            for u in range(UNROLL):
                one(group * UNROLL + u)


def beam_partials(samples, weights, usable, table, groups):
    _, _, antennas, times, subbands = samples.shape
    beams = weights.shape[2]
    steps = antennas // ANTENNAS_PER_STEP
    w_step = beams // steps
    grid_spec = pltpu.PrefetchScalarGridSpec(
        num_scalar_prefetch=1,
        grid=(subbands // LANES, steps),
        in_specs=[
            pl.BlockSpec((2, 1, ANTENNAS_PER_STEP, times, LANES), lambda f, s, *_: (0, 0, s, 0, f)),
            pl.BlockSpec((2, 1, w_step, antennas, LANES), lambda f, s, *_: (0, 0, s, 0, f)),
            pl.BlockSpec((1, antennas), lambda f, s, *_: (0, 0)),
        ],
        out_specs=[
            pl.BlockSpec((subbands, 2 * beams, times), lambda f, s, *_: (0, 0, 0)),
            pl.BlockSpec((subbands // groups + 1, 2 * beams, times), lambda f, s, *_: (0, 0, 0)),
        ],
        scratch_shapes=[
            pltpu.SMEM((subbands,), jnp.int32),
            pltpu.VMEM((LANES * (2 * antennas + 8), times), jnp.float32),
            pltpu.VMEM((LANES * (2 * beams + 8), LANES), jnp.float32),
        ],
    )
    return pl.pallas_call(
        functools.partial(beam_kernel, antennas=antennas, beams=beams),
        grid_spec=grid_spec,
        out_shape=[
            jax.ShapeDtypeStruct((subbands, 2 * beams, times), jnp.bfloat16),
            jax.ShapeDtypeStruct((subbands // groups + 1, 2 * beams, times), jnp.float32),
        ],
        compiler_params=pltpu.CompilerParams(
            dimension_semantics=("arbitrary", "arbitrary"), vmem_limit_bytes=60 * 1024 * 1024
        ),
    )(table, samples, weights, usable)


def exchange_kernel(
    sent_ref, own_hbm, count_ref, out_ref,
    own, arrived, outgoing, gathered, sums, returned, counts,
    own_sem, count_send, count_recv, chan_send, chan_recv, beam_send, beam_recv, back_send, back_recv,
):
    groups, stations = lax.axis_size("chan"), lax.axis_size("station")
    mine, me = lax.axis_index("chan"), lax.axis_index("station")
    phases, _, depth, rows, times = gathered.shape
    beams = rows // 2
    kept = own.shape[0]
    share = phases * depth
    wide = min(STATIONS_PER_STEP, stations)
    pieces = stations // wide

    def target(k):
        return lax.rem(me + stations // 2 + ((k + 1) // 2) * (1 - 2 * lax.rem(k, 2)), stations)

    def remote(src, dst, send, recv, device):
        return pltpu.make_async_remote_copy(
            src_ref=src, dst_ref=dst, send_sem=send, recv_sem=recv,
            device_id=device, device_id_type=pl.DeviceIdType.MESH,
        )

    def chan_copy(g, p, k):
        peer = lax.rem(mine + g, groups)
        start = peer * kept + target(k) * share + p * depth
        return remote(
            sent_ref.at[pl.ds(start, depth)], arrived.at[g - 1, p, k],
            chan_send.at[g - 1, p, k], chan_recv.at[g - 1, p, k], (me, peer),
        )

    def count_copy(g):
        return remote(
            count_ref, counts.at[g - 1], count_send.at[g - 1], count_recv.at[g - 1], (me, lax.rem(mine + g, groups))
        )

    def beam_copy(p, k):
        return remote(outgoing.at[p, k], gathered.at[p, me], beam_send.at[p, k], beam_recv.at[p, k], (target(k), mine))

    def back_copy(p, k):
        there = target(k)
        return remote(
            sums.at[p, pl.ds(pl.multiple_of(there * beams, beams), beams)],
            returned.at[p, me], back_send.at[p, k], back_recv.at[p, k], (there, mine),
        )

    load = pltpu.make_async_copy(own_hbm.at[pl.ds(0, kept)], own, own_sem)
    load.start()
    barrier = pltpu.get_barrier_semaphore()
    for g in range(1, groups):
        pl.semaphore_signal(
            barrier, inc=1, device_id=(me, lax.rem(mine + g, groups)), device_id_type=pl.DeviceIdType.MESH
        )

    @pl.loop(0, stations - 1)
    def _(k):
        pl.semaphore_signal(barrier, inc=1, device_id=(target(k), mine), device_id_type=pl.DeviceIdType.MESH)

    pl.semaphore_wait(barrier, groups - 1 + stations - 1)

    for g in range(1, groups):
        count_copy(g).start()
    for p in range(phases):
        @pl.loop(0, stations)
        def _(k):
            for g in range(1, groups):
                chan_copy(g, p, k).start()

    sums[...] = jnp.zeros_like(sums)
    load.wait()
    count = count_ref[...]
    for g in range(1, groups):
        count_copy(g).wait_recv()
        count = count + counts[g - 1]
    gain = lax.rsqrt(count)[0:1, :times].reshape(1, 1, times)

    def chunk(p, k):
        start = target(k) * share + p * depth
        total = own[pl.ds(start, depth)]
        for g in range(1, groups):
            chan_copy(g, p, k).wait_recv()
            total = total + arrived[g - 1, p, k].astype(jnp.float32)
        return (total * gain).astype(jnp.bfloat16)

    def forward(p, k):
        outgoing[p, k] = chunk(p, k)
        beam_copy(p, k).start()

    def forward_range(p, first, last, extra=None):
        @pl.loop(first, last)
        def _(k):
            forward(p, k)
            if extra is not None:
                extra(k)

    def keep(p):
        gathered[p, me] = chunk(p, stations - 1)

    def await_beams(p):
        @pl.loop(0, stations - 1)
        def _(k):
            beam_copy(p, k).wait_recv()

    columns = stations * beams
    lanes = sums.shape[2]

    def correlate(p, index):
        j, piece = index // pieces, lax.rem(index, pieces)

        def beams_of(stations_slice, count, part):
            return gathered[p, stations_slice, j, pl.ds(part * beams, beams), :].reshape(count * beams, times)

        some = pl.ds(piece * wide, wide)
        x_re, x_im = beams_of(some, wide, 0), beams_of(some, wide, 1)
        every = pl.ds(0, stations)
        y = jnp.concatenate([beams_of(every, stations, 0), beams_of(every, stations, 1)], axis=1)
        same = lax.rem(lax.broadcasted_iota(jnp.int32, (wide * beams, columns), 0), beams) == lax.rem(
            lax.broadcasted_iota(jnp.int32, (wide * beams, columns), 1), beams
        )
        station_of = lax.broadcasted_iota(jnp.int32, (columns, lanes), 0) // beams
        lane = lax.broadcasted_iota(jnp.int32, (columns, lanes), 1)
        where = pl.ds(pl.multiple_of(piece * (wide * beams), wide * beams), wide * beams)
        total = sums[p, where, :]
        for part, x in enumerate((jnp.concatenate([x_re, x_im], axis=1), jnp.concatenate([x_im, -x_re], axis=1))):
            pairs = lax.dot_general(x, y, (((1,), (1,)), ((), ())), preferred_element_type=jnp.float32)
            high, low = split(jnp.where(same, pairs, 0.0))
            place = (lane == station_of + (j * 2 + part) * stations).astype(jnp.float32).astype(jnp.bfloat16)
            total = total + (
                jnp.dot(high, place, preferred_element_type=jnp.float32)
                + jnp.dot(low, place, preferred_element_type=jnp.float32)
            )
        sums[p, where, :] = total

    def send_back(p):
        @pl.loop(0, stations - 1)
        def _(k):
            back_copy(p, k).start()

        returned[p, me] = sums[p, pl.ds(pl.multiple_of(me * beams, beams), beams), :]

    last = phases - 1
    for p in range(phases):
        if p == 0:
            forward_range(p, 0, stations - 1)
        else:
            quarter, half = stations // 4, stations // 2
            each = depth * pieces // half
            forward_range(p, 0, quarter)
            await_beams(p - 1)

            def extra(k):
                for c in range(each):
                    correlate(p - 1, (k - quarter) * each + c)

            forward_range(p, quarter, quarter + half, extra)
            send_back(p - 1)
            forward_range(p, quarter + half, stations - 1)
        keep(p)
    await_beams(last)

    @pl.loop(0, depth * pieces)
    def _(index):
        correlate(last, index)

    send_back(last)
    for p in range(phases):
        @pl.loop(0, stations - 1)
        def _(k):
            back_copy(p, k).wait_recv()
    out_ref[...] = returned[...]
    for g in range(1, groups):
        count_copy(g).wait_send()
    for p in range(phases):
        @pl.loop(0, stations)
        def _(k):
            for g in range(1, groups):
                chan_copy(g, p, k).wait_send()

        @pl.loop(0, stations - 1)
        def _(k):
            beam_copy(p, k).wait_send()
            back_copy(p, k).wait_send()


def exchange(sent, own, count, beams, groups, stations):
    subbands, rows, times = sent.shape
    kept = subbands // groups
    share = kept // stations
    phases = 2 if share % 4 == 0 else 1
    depth = share // phases
    lanes = depth * 2 * stations
    dma = pltpu.SemaphoreType.DMA
    return pl.pallas_call(
        exchange_kernel,
        out_shape=jax.ShapeDtypeStruct((phases, stations, beams, lanes), jnp.float32),
        in_specs=[
            pl.BlockSpec(memory_space=pl.ANY),
            pl.BlockSpec(memory_space=pl.ANY),
            pl.BlockSpec(memory_space=pltpu.VMEM),
        ],
        out_specs=pl.BlockSpec(memory_space=pltpu.VMEM),
        scratch_shapes=[
            pltpu.VMEM((kept, rows, times), jnp.float32),
            pltpu.VMEM((groups - 1, phases, stations, depth, rows, times), jnp.bfloat16),
            pltpu.VMEM((phases, stations, depth, rows, times), jnp.bfloat16),
            pltpu.VMEM((phases, stations, depth, rows, times), jnp.bfloat16),
            pltpu.VMEM((phases, stations * beams, lanes), jnp.float32),
            pltpu.VMEM((phases, stations, beams, lanes), jnp.float32),
            pltpu.VMEM((groups - 1, 8, LANES), jnp.float32),
            dma,
            dma((groups - 1,)),
            dma((groups - 1,)),
            dma((groups - 1, phases, stations)),
            dma((groups - 1, phases, stations)),
            dma((phases, stations)),
            dma((phases, stations)),
            dma((phases, stations)),
            dma((phases, stations)),
        ],
        compiler_params=pltpu.CompilerParams(
            collective_id=0, has_side_effects=True, vmem_limit_bytes=62 * 1024 * 1024
        ),
    )(sent, own, count)


def on_device(samples, weights, antenna_flags, subband_table):
    usable = antenna_flags.astype(jnp.float32)
    groups, stations = lax.axis_size("chan"), lax.axis_size("station")
    beams = weights.shape[2]
    sent, own = beam_partials(samples, weights, usable, subband_table, groups)
    count = jnp.broadcast_to(jnp.sum(usable, axis=1)[:, None], (8, LANES))
    back = exchange(sent, own, count, beams, groups, stations)
    phases = back.shape[0]
    back = back.reshape(phases, stations, beams, -1, 2, stations)
    back = back.transpose(1, 0, 3, 4, 2, 5)
    return back.reshape(-1, 2, 1, beams, stations)


def solution(mesh):
    in_specs = (
        P(None, "station", "chan", None, None),
        P(None, "station", None, "chan", None),
        P("station", "chan"),
        P(),
    )
    out_specs = P("chan", None, "station", None, None)
    return jax.shard_map(
        on_device, mesh=mesh, in_specs=in_specs, out_specs=out_specs, check_vma=False
    )
```

profile of v0, /device:TPU:0, one launch (start us, length us, event | category | flops | bytes accessed | tf_op | source)
XLA Modules:
  0.0 119.9 jit_solution(16673984818898039512)
XLA Ops:
  0.0 1.3 %convert_reduce_fusion = f32[]{:T(128)} fusion(s32[1,128]{1,0:T(1,128)} %param.6), kind=kLoop, calls=%fused_computation | loop fusion | flops 255 | bytes 516 | tf_op jit(solution)/shard_map/reduce_sum | solution.py:342
  1.3 1.2 convert_element_type.3.usable_ref
  2.5 1.3 %broadcast_in_dim.2.count_ref = f32[8,128]{1,0:T(8,128)} broadcast(f32[]{:T(128)} %convert_reduce_fusion), dimensions={} | broadcast | bytes 4100 | tf_op jit(solution)/shard_map/broadcast_in_dim | solution.py:342
  3.8 32.1 %shard_map.46 = (bf16[256,64,128]{2,1,0:T(8,128)(2,1)}, f32[129,64,128]{2,1,0:T(8,128)}) custom-call(s32[256]{0:T(256)} %table_ref.1, f32[2,1,128,128,256]{4,3,2,1,0:T(8,128)} %x_ref.1, f32[2,1,32,128,256]{4,3,2,1,0:T(8,128)} %w_ref.1, f32[1,128]{1,0:T(1,128)} %convert_element_type.3.usable_ref), custom_call_target="tpu_custom_call" | custom-call | tf_op jit(solution)/shard_map/pallas_call | solution.py:99
  35.9 80.2 %shard_map.47 = f32[2,16,32,128]{3,2,1,0:T(8,128)} custom-call(bf16[256,64,128]{2,1,0:T(8,128)(2,1)} %get-tuple-element.7.sent_ref, f32[129,64,128]{2,1,0:T(8,128)} %get-tuple-element.8.own_hbm, f32[8,128]{1,0:T(8,128)} %broadcast_in_dim.2.count_ref), custom_call_target="tpu_custom_call" | custom-call | tf_op jit(solution)/shard_map/pallas_call | solution.py:304
  116.1 1.6 %copy.9 = f32[2,16,32,128]{2,3,0,1:T(8,128)S(1)} copy(f32[2,16,32,128]{3,2,1,0:T(8,128)} %shard_map.47) | data formatting | bytes 1048576 | tf_op jit(solution)/shard_map/transpose | solution.py:346
  117.8 2.2 %copy.8 = f32[128,2,1,32,16]{0,4,3,2,1:T(8,128)} copy(f32[128,2,1,32,16]{3,4,1,0,2:T(8,128)S(1)} %bitcast.5) | data formatting | bytes 1048576 | tf_op jit(solution)/shard_map/reshape | solution.py:347
where the time goes:
time: 120 us
  Pallas kernels  112 us (93%)
  local copies, waits for them, and re-layouts  5.11 us (4%)
  other arithmetic  2.51 us (2%)
    pallas_call x1, Pallas kernels, exchange(): pl.pallas_call(exchange_kernel, out_shape=jax.ShapeDtypeStruct((phases, s...  80.2 us
    pallas_call x1, Pallas kernels, beam_partials(): pl.pallas_call(functools.partial(beam_kernel, antennas=antennas, beams=be...  32.1 us

commit v1 on v0

v1 whole, which is shorter than its diff:
```python
import functools

import jax
import jax.numpy as jnp
from jax import lax
from jax.experimental import pallas as pl
from jax.experimental.pallas import tpu as pltpu
from jax.sharding import PartitionSpec as P

LANES = 128
SLAB = 64
SLABS_PER_CHUNK = 8
CHUNKS_IN_FLIGHT = 8
GROUP = 4
TILE_BEAMS = 16


def split(value):
    high = value.astype(jnp.bfloat16)
    low = (value - high.astype(jnp.float32)).astype(jnp.bfloat16)
    return high, low


def kernel(
    table_ref, flags_ref, x_hbm, w_hbm, out_ref,
    x_rows, w_rows, chunk_buf, own, partials, arrived, gathered, results, returned, count_ref, counts,
    chunk_sem, count_send, count_recv, chan_send, chan_recv, beam_send, beam_recv, back_send, back_recv,
):
    groups, stations = lax.axis_size("chan"), lax.axis_size("station")
    mine, me = lax.axis_index("chan"), lax.axis_index("station")
    halves, share = gathered.shape[0], gathered.shape[1]
    antennas = x_hbm.shape[2]
    subbands = x_hbm.shape[4]
    beams = gathered.shape[3]
    kept = subbands // groups
    blocks = subbands // LANES
    tall = min(antennas, SLAB)
    x_stride = x_rows.shape[2]
    w_stride = w_rows.shape[1]
    w_chunks = w_hbm.shape[2] // SLABS_PER_CHUNK
    x_chunks = antennas // SLABS_PER_CHUNK
    chunks = w_chunks + halves * x_chunks
    beams_per_chunk = SLABS_PER_CHUNK * SLAB // antennas
    parts_of_phase = stations // GROUP
    x_lines = x_rows.reshape(halves, subbands * x_stride, LANES)
    w_lines = w_rows.reshape(subbands * w_stride, LANES)

    def target(k):
        return lax.rem(me + stations // 2 + ((k + 1) // 2) * (1 - 2 * lax.rem(k, 2)), stations)

    def remote(src, dst, send, recv, device):
        return pltpu.make_async_remote_copy(
            src_ref=src, dst_ref=dst, send_sem=send, recv_sem=recv,
            device_id=device, device_id_type=pl.DeviceIdType.MESH,
        )

    def chan_copy(g, h, i, q):
        peer = lax.rem(mine + g, groups)
        return remote(
            partials.at[g - 1, h, i, q], arrived.at[g - 1, h, i, q],
            chan_send.at[g - 1, h, i, q], chan_recv.at[g - 1, h, i, q], (me, peer),
        )

    def count_copy(g):
        return remote(
            count_ref, counts.at[g - 1], count_send.at[g - 1], count_recv.at[g - 1], (me, lax.rem(mine + g, groups))
        )

    def beam_copy(h, i, q, u):
        k = q * GROUP + u
        return remote(
            arrived.at[0, h, i, q, u], gathered.at[h, i, me],
            beam_send.at[h, i, k], beam_recv.at[h, i, k], (target(k), mine),
        )

    def back_copy(i, k):
        there = target(k)
        return remote(
            results.at[i, there], returned.at[i * stations + me],
            back_send.at[i, k], back_recv.at[i, k], (there, mine),
        )

    def w_copy(n, slot):
        return pltpu.make_async_copy(
            w_hbm.at[:, 0, pl.ds(n * SLABS_PER_CHUNK, SLABS_PER_CHUNK)], chunk_buf.at[slot], chunk_sem.at[slot]
        )

    def x_copy(n, slot):
        half = n // x_chunks
        first = lax.rem(n, x_chunks) * SLABS_PER_CHUNK
        return pltpu.make_async_copy(
            x_hbm.at[:, 0, pl.ds(first, SLABS_PER_CHUNK), pl.ds(half * SLAB, SLAB)],
            chunk_buf.at[slot], chunk_sem.at[slot],
        )

    def slot_of(n):
        return lax.rem(n, CHUNKS_IN_FLIGHT)

    def start_chunk(n):
        @pl.when(n < w_chunks)
        def _():
            w_copy(n, slot_of(n)).start()

        @pl.when((n >= w_chunks) & (n < chunks))
        def _():
            x_copy(n - w_chunks, slot_of(n)).start()

    for n in range(min(CHUNKS_IN_FLIGHT, chunks)):
        if n < w_chunks:
            w_copy(n, n % CHUNKS_IN_FLIGHT).start()
        else:
            x_copy(n - w_chunks, n % CHUNKS_IN_FLIGHT).start()

    barrier = pltpu.get_barrier_semaphore()
    for g in range(1, groups):
        pl.semaphore_signal(
            barrier, inc=1, device_id=(me, lax.rem(mine + g, groups)), device_id_type=pl.DeviceIdType.MESH
        )

    @pl.loop(0, stations - 1)
    def _(k):
        pl.semaphore_signal(barrier, inc=1, device_id=(target(k), mine), device_id_type=pl.DeviceIdType.MESH)

    usable = flags_ref[...].astype(jnp.float32)
    count_ref[...] = jnp.broadcast_to(jnp.sum(usable, axis=1, keepdims=True), count_ref.shape)
    if antennas < LANES:
        usable = jnp.concatenate([usable, jnp.zeros((1, LANES - antennas), jnp.float32)], axis=1)

    @pl.loop(0, w_chunks)
    def _(n):
        slot = slot_of(n)
        w_copy(n, slot).wait()
        for part in range(2):
            for b in range(beams_per_chunk):
                for block in range(blocks):
                    lanes = slice(block * LANES, (block + 1) * LANES)
                    tiles = [
                        chunk_buf[slot, part, row // SLAB, row % SLAB : row % SLAB + tall, lanes]
                        for row in range(b * antennas, (b + 1) * antennas, tall)
                    ]
                    if antennas < LANES:
                        tiles.append(jnp.zeros((LANES - antennas, LANES), jnp.float32))
                    row = block * LANES * w_stride + part * beams + n * beams_per_chunk + b
                    w_lines[pl.ds(row, LANES, stride=w_stride), :] = jnp.concatenate(tiles, axis=0).T * usable
        start_chunk(n + CHUNKS_IN_FLIGHT)

    def turn(h, first, last):
        @pl.loop(first, last)
        def _(m):
            n = w_chunks + h * x_chunks + m
            slot = slot_of(n)
            x_copy(h * x_chunks + m, slot).wait()
            for a in range(SLABS_PER_CHUNK):
                for block in range(blocks):
                    lanes = pl.ds(block * LANES, LANES)
                    tile = jnp.concatenate([chunk_buf[slot, part, a, :, lanes] for part in range(2)], axis=0)
                    row = block * LANES * x_stride + m * SLABS_PER_CHUNK + a
                    x_lines[h, pl.ds(row, LANES, stride=x_stride), :] = tile.T
            start_chunk(n + CHUNKS_IN_FLIGHT)

    turn(0, 0, x_chunks)

    pl.semaphore_wait(barrier, groups - 1 + stations - 1)
    for g in range(1, groups):
        count_copy(g).start()

    lane = lax.broadcasted_iota(jnp.int32, (beams, LANES), 1)
    sign = jnp.where(lane < SLAB, -1.0, 1.0).astype(jnp.float32)

    def partial(h, slot):
        f = table_ref[slot]
        x = x_rows[h, f, :antennas, :]
        w = w_rows[f, : 2 * beams, :antennas]
        x_pair = jnp.concatenate(split(x), axis=0)
        w_high, w_low = split(w)
        grid = jnp.dot(
            jnp.concatenate([w_high, w_high], axis=1), x_pair, preferred_element_type=jnp.float32
        ) + jnp.dot(jnp.concatenate([w_low, w_low], axis=1), x_pair, preferred_element_type=jnp.float32)
        return grid[:beams] + pltpu.roll(grid[beams:], SLAB, axis=1) * sign

    def peers(h, i):
        for g in range(1, groups):
            first = lax.rem(mine + g, groups) * kept + i * stations

            @pl.loop(0, parts_of_phase)
            def _(q):
                for u in range(GROUP):
                    total = partial(h, first + target(q * GROUP + u))
                    partials[g - 1, h, i, q, u] = total.astype(jnp.bfloat16)
                chan_copy(g, h, i, q).start()

    def own_sums(h, i):
        first = mine * kept + i * stations

        @pl.loop(0, parts_of_phase)
        def _(q):
            for u in range(GROUP):
                own[q, u] = partial(h, first + target(q * GROUP + u))

    def forward(h, i, gain):
        def piece(q, last):
            for g in range(1, groups):
                chan_copy(g, h, i, q).wait_recv()
            for u in range(GROUP):
                total = own[q, u]
                for g in range(1, groups):
                    total = total + arrived[g - 1, h, i, q, u].astype(jnp.float32)
                value = (total * gain).astype(jnp.bfloat16)
                if last and u == GROUP - 1:
                    gathered[h, i, me] = value
                else:
                    arrived[0, h, i, q, u] = value
                    beam_copy(h, i, q, u).start()

        @pl.loop(0, parts_of_phase - 1)
        def _(q):
            piece(q, False)

        piece(parts_of_phase - 1, True)

    tile_rows = stations * TILE_BEAMS
    mask = lax.broadcasted_iota(jnp.int32, (TILE_BEAMS, tile_rows), 0) == lax.rem(
        lax.broadcasted_iota(jnp.int32, (TILE_BEAMS, tile_rows), 1), TILE_BEAMS
    )
    chosen = mask.astype(jnp.float32).reshape(1, TILE_BEAMS, tile_rows)
    wide = tile_rows // LANES
    beam_tiles = beams // TILE_BEAMS
    result_rows = 2 * beam_tiles * wide

    def correlate(i):
        for h in range(halves):
            @pl.loop(0, stations - 1)
            def _(k):
                beam_copy(h, i, k // GROUP, lax.rem(k, GROUP)).wait_recv()

        for tile in range(beam_tiles):
            straight, turned = [], []
            for h in range(halves):
                y = gathered[h, i, :, pl.ds(tile * TILE_BEAMS, TILE_BEAMS), :].reshape(tile_rows, LANES)
                straight.append(y)
                swapped = jnp.concatenate([y[:, SLAB:], -y[:, :SLAB]], axis=1)
                turned.append(swapped)
            y = jnp.concatenate(straight, axis=1)
            for part, x in enumerate((y, jnp.concatenate(turned, axis=1))):
                pairs = lax.dot_general(x, y, (((1,), (1,)), ((), ())), preferred_element_type=jnp.float32)
                total = jnp.sum(pairs.reshape(stations, TILE_BEAMS, tile_rows) * chosen, axis=1)
                for piece in range(wide):
                    row = (part * beam_tiles + tile) * wide + piece
                    results[i, :, row, :] = total[:, piece * LANES : (piece + 1) * LANES]

        @pl.loop(0, stations - 1)
        def _(k):
            back_copy(i, k).start()

        returned[i * stations + me] = results[i, me]

    peers(0, 0)
    count = count_ref[...]
    for g in range(1, groups):
        count_copy(g).wait_recv()
        count = count + counts[g - 1]
    gain = lax.rsqrt(count)[0:1, :]

    each = x_chunks // share
    for h in range(halves):
        @pl.loop(0, share)
        def _(i):
            own_sums(h, i)
            if h + 1 < halves:
                turn(h + 1, i * each, (i + 1) * each)

            @pl.when(i + 1 < share)
            def _():
                peers(h, i + 1)

            if h + 1 < halves:
                @pl.when(i + 1 == share)
                def _():
                    peers(h + 1, 0)

            forward(h, i, gain)
            if h + 1 == halves:
                @pl.when(i > 0)
                def _():
                    correlate(i - 1)

    correlate(share - 1)

    @pl.loop(0, share)
    def _(i):
        @pl.loop(0, stations - 1)
        def _(k):
            back_copy(i, k).wait_recv()

    per_row = LANES // TILE_BEAMS
    for part in range(2):
        for tile in range(beam_tiles):
            for piece in range(wide):
                row = (part * beam_tiles + tile) * wide + piece
                turned = returned[:, row, :].T
                for r in range(per_row):
                    out_ref[part, pl.ds(tile * TILE_BEAMS, TILE_BEAMS), piece * per_row + r, :] = turned[
                        r * TILE_BEAMS : (r + 1) * TILE_BEAMS
                    ]

    for g in range(1, groups):
        count_copy(g).wait_send()
    for h in range(halves):
        @pl.loop(0, share)
        def _(i):
            @pl.loop(0, parts_of_phase)
            def _(q):
                for g in range(1, groups):
                    chan_copy(g, h, i, q).wait_send()

            @pl.loop(0, stations - 1)
            def _(k):
                beam_copy(h, i, k // GROUP, lax.rem(k, GROUP)).wait_send()

    @pl.loop(0, share)
    def _(i):
        @pl.loop(0, stations - 1)
        def _(k):
            back_copy(i, k).wait_send()


def on_device(samples, weights, antenna_flags, subband_table):
    groups, stations = lax.axis_size("chan"), lax.axis_size("station")
    _, _, antennas, times, subbands = samples.shape
    beams = weights.shape[2]
    kept = subbands // groups
    share = kept // stations
    halves = times // SLAB
    quarters = stations // GROUP
    rows = 2 * (beams // TILE_BEAMS) * (stations * TILE_BEAMS // LANES)
    slabs = weights.reshape(2, 1, beams * antennas // SLAB, SLAB, subbands)
    dma = pltpu.SemaphoreType.DMA
    out = pl.pallas_call(
        kernel,
        out_shape=jax.ShapeDtypeStruct((2, beams, stations, kept), jnp.float32),
        in_specs=[
            pl.BlockSpec(memory_space=pltpu.SMEM),
            pl.BlockSpec(memory_space=pltpu.VMEM),
            pl.BlockSpec(memory_space=pl.ANY),
            pl.BlockSpec(memory_space=pl.ANY),
        ],
        out_specs=pl.BlockSpec(memory_space=pltpu.VMEM),
        scratch_shapes=[
            pltpu.VMEM((halves, subbands, antennas + 8, LANES), jnp.float32),
            pltpu.VMEM((subbands, 2 * beams + 8, LANES), jnp.float32),
            pltpu.VMEM((CHUNKS_IN_FLIGHT, 2, SLABS_PER_CHUNK, SLAB, subbands), jnp.float32),
            pltpu.VMEM((quarters, GROUP, beams, LANES), jnp.float32),
            pltpu.VMEM((groups - 1, halves, share, quarters, GROUP, beams, LANES), jnp.bfloat16),
            pltpu.VMEM((groups - 1, halves, share, quarters, GROUP, beams, LANES), jnp.bfloat16),
            pltpu.VMEM((halves, share, stations, beams, LANES), jnp.bfloat16),
            pltpu.VMEM((share, stations, rows, LANES), jnp.float32),
            pltpu.VMEM((kept, rows, LANES), jnp.float32),
            pltpu.VMEM((8, LANES), jnp.float32),
            pltpu.VMEM((groups - 1, 8, LANES), jnp.float32),
            dma((CHUNKS_IN_FLIGHT,)),
            dma((groups - 1,)),
            dma((groups - 1,)),
            dma((groups - 1, halves, share, quarters)),
            dma((groups - 1, halves, share, quarters)),
            dma((halves, share, stations)),
            dma((halves, share, stations)),
            dma((share, stations)),
            dma((share, stations)),
        ],
        compiler_params=pltpu.CompilerParams(
            collective_id=0, has_side_effects=True, vmem_limit_bytes=67043328
        ),
    )(subband_table, antenna_flags, samples, slabs)
    return out.transpose(3, 0, 1, 2)[:, :, None]


def solution(mesh):
    in_specs = (
        P(None, "station", "chan", None, None),
        P(None, "station", None, "chan", None),
        P("station", "chan"),
        P(),
    )
    out_specs = P("chan", None, "station", None, None)
    return jax.shard_map(
        on_device, mesh=mesh, in_specs=in_specs, out_specs=out_specs, check_vma=False
    )
```

time: 120 us -> 103 us (0.86)
  Pallas kernels: 112 us -> 102 us
  local copies, waits for them, and re-layouts: 5.11 us -> 1.87 us
  other arithmetic: 2.51 us -> 0 us
    pallas_call x2 -> x1, Pallas kernels: 112 us -> 102 us  [on_device(): pl.pallas_call(kernel, out_shape=jax.ShapeDtypeStruct((2, beams, stations...]
    reshape x1 -> x0, local copies, waits for them, and re-layouts: 2.18 us -> none  [on_device(): return back.reshape(-1, 2, 1, beams, stations)]
    unnamed x0 -> x1, local copies, waits for them, and re-layouts: none -> 1.87 us
    transpose x1 -> x0, local copies, waits for them, and re-layouts: 1.65 us -> none  [on_device(): back = back.transpose(1, 0, 3, 4, 2, 5)]
    reduce_sum x1 -> x0, other arithmetic: 1.34 us -> none  [on_device(): count = jnp.broadcast_to(jnp.sum(usable, axis=1)[:, None], (8, LANES))]
    broadcast_in_dim x1 -> x0, local copies, waits for them, and re-layouts: 1.28 us -> none  [on_device(): count = jnp.broadcast_to(jnp.sum(usable, axis=1)[:, None], (8, LANES))]
where the time goes in v1:
time: 103 us
  Pallas kernels  102 us (99%)
  local copies, waits for them, and re-layouts  1.87 us (2%)
    pallas_call x1, Pallas kernels, on_device(): pl.pallas_call(kernel, out_shape=jax.ShapeDtypeStruct((2, beams, stations...  102 us

profile of v1, /device:TPU:0, one launch (start us, length us, event | category | flops | bytes accessed | tf_op | source)
XLA Modules:
  0.0 103.4 jit_solution(18171945854073403124)
XLA Ops:
  0.0 101.6 %shard_map.46 = f32[2,32,16,128]{3,2,1,0:T(8,128)} custom-call(s32[256]{0:T(256)} %table_ref.1, s32[1,128]{1,0:T(1,128)} %flags_ref.1, f32[2,1,128,128,256]{4,3,2,1,0:T(8,128)} %x_hbm.1, f32[2,1,64,64,256]{4,3,2,1,0:T(8,128)} %bitcast.6), custom_call_target="tpu_custom_call" | custom-call | tf_op jit(solution)/shard_map/pallas_call | solution.py:338
  101.6 1.9 %copy.7 = f32[128,2,1,32,16]{0,4,3,2,1:T(8,128)} copy(f32[128,2,1,32,16]{0,4,3,2,1:T(8,128)} %bitcast.7) | data formatting | bytes 1048576

commit v2 on v1

--- a/solution.py
+++ b/solution.py
@@ -11,7 +11,7 @@
 SLAB = 64
 SLABS_PER_CHUNK = 8
 CHUNKS_IN_FLIGHT = 8
-GROUP = 4
+GROUP = 8
 TILE_BEAMS = 16
 
 
@@ -58,7 +58,7 @@
         peer = lax.rem(mine + g, groups)
         return remote(
             partials.at[g - 1, h, i, q], arrived.at[g - 1, h, i, q],
-            chan_send.at[g - 1, h, i, q], chan_recv.at[g - 1, h, i, q], (me, peer),
+            chan_send, chan_recv.at[g - 1, h, i, q], (me, peer),
         )
 
     def count_copy(g):
@@ -67,18 +67,22 @@
         )
 
     def beam_copy(h, i, q, u):
-        k = q * GROUP + u
         return remote(
             arrived.at[0, h, i, q, u], gathered.at[h, i, me],
-            beam_send.at[h, i, k], beam_recv.at[h, i, k], (target(k), mine),
+            beam_send, beam_recv.at[i], (target(q * GROUP + u), mine),
         )
 
     def back_copy(i, k):
         there = target(k)
         return remote(
             results.at[i, there], returned.at[i * stations + me],
-            back_send.at[i, k], back_recv.at[i, k], (there, mine),
-        )
+            back_send, back_recv, (there, mine),
+        )
+
+    def all_of(ref, send, recv):
+        return remote(ref, ref, send, recv, (me, lax.rem(mine + 1, groups)))
+
+    others = pl.ds(0, stations - 1)
 
     def w_copy(n, slot):
         return pltpu.make_async_copy(
@@ -228,11 +232,7 @@
     result_rows = 2 * beam_tiles * wide
 
     def correlate(i):
-        for h in range(halves):
-            @pl.loop(0, stations - 1)
-            def _(k):
-                beam_copy(h, i, k // GROUP, lax.rem(k, GROUP)).wait_recv()
-
+        all_of(gathered.at[:, i, others], beam_send, beam_recv.at[i]).wait_recv()
         for tile in range(beam_tiles):
             straight, turned = [], []
             for h in range(halves):
@@ -286,11 +286,7 @@
 
     correlate(share - 1)
 
-    @pl.loop(0, share)
-    def _(i):
-        @pl.loop(0, stations - 1)
-        def _(k):
-            back_copy(i, k).wait_recv()
+    all_of(returned.at[pl.ds(0, share * (stations - 1))], back_send, back_recv).wait_recv()
 
     per_row = LANES // TILE_BEAMS
     for part in range(2):
@@ -305,23 +301,9 @@
 
     for g in range(1, groups):
         count_copy(g).wait_send()
-    for h in range(halves):
-        @pl.loop(0, share)
-        def _(i):
-            @pl.loop(0, parts_of_phase)
-            def _(q):
-                for g in range(1, groups):
-                    chan_copy(g, h, i, q).wait_send()
-
-            @pl.loop(0, stations - 1)
-            def _(k):
-                beam_copy(h, i, k // GROUP, lax.rem(k, GROUP)).wait_send()
-
-    @pl.loop(0, share)
-    def _(i):
-        @pl.loop(0, stations - 1)
-        def _(k):
-            back_copy(i, k).wait_send()
+    all_of(partials, chan_send, chan_recv.at[0, 0, 0, 0]).wait_send()
+    all_of(gathered.at[:, :, others], beam_send, beam_recv.at[0]).wait_send()
+    all_of(results.at[:, others], back_send, back_recv).wait_send()
 
 
 def on_device(samples, weights, antenna_flags, subband_table):
@@ -360,12 +342,12 @@
             dma((CHUNKS_IN_FLIGHT,)),
             dma((groups - 1,)),
             dma((groups - 1,)),
+            dma,
             dma((groups - 1, halves, share, quarters)),
-            dma((groups - 1, halves, share, quarters)),
-            dma((halves, share, stations)),
-            dma((halves, share, stations)),
-            dma((share, stations)),
-            dma((share, stations)),
+            dma,
+            dma((share,)),
+            dma,
+            dma,
         ],
         compiler_params=pltpu.CompilerParams(
             collective_id=0, has_side_effects=True, vmem_limit_bytes=67043328

time: 103 us -> 88.4 us (0.86)
  Pallas kernels: 102 us -> 86.3 us
    pallas_call x1, Pallas kernels: 102 us -> 86.3 us  [on_device(): pl.pallas_call(kernel, out_shape=jax.ShapeDtypeStruct((2, beams, stations...]
where the time goes in v2:
time: 88.4 us; the launch traced here: 88.2 us
  Pallas kernels  86.3 us (98%)
  local copies, waits for them, and re-layouts  1.87 us (2%)
    pallas_call x1, Pallas kernels, on_device(): pl.pallas_call(kernel, out_shape=jax.ShapeDtypeStruct((2, beams, stations...  86.3 us
    unnamed x1, local copies, waits for them, and re-layouts  1.87 us

profile of v2, /device:TPU:0, one launch (start us, length us, event | category | flops | bytes accessed | tf_op | source)
XLA Modules:
  0.0 88.2 jit_solution(1555857965374052408)
XLA Ops:
  0.0 86.3 %shard_map.46 = f32[2,32,16,128]{3,2,1,0:T(8,128)} custom-call(s32[256]{0:T(256)} %table_ref.1, s32[1,128]{1,0:T(1,128)} %flags_ref.1, f32[2,1,128,128,256]{4,3,2,1,0:T(8,128)} %x_hbm.1, f32[2,1,64,64,256]{4,3,2,1,0:T(8,128)} %bitcast.6), custom_call_target="tpu_custom_call" | custom-call | tf_op jit(solution)/shard_map/pallas_call | solution.py:320
  86.3 1.9 %copy.7 = f32[128,2,1,32,16]{0,4,3,2,1:T(8,128)} copy(f32[128,2,1,32,16]{0,4,3,2,1:T(8,128)} %bitcast.7) | data formatting | bytes 1048576

commit v3 on v2

--- a/solution.py
+++ b/solution.py
@@ -13,6 +13,8 @@
 CHUNKS_IN_FLIGHT = 8
 GROUP = 8
 TILE_BEAMS = 16
+AHEAD = 3
+BEHIND = 3
 
 
 def split(value):
@@ -23,8 +25,9 @@
 
 def kernel(
     table_ref, flags_ref, x_hbm, w_hbm, out_ref,
-    x_rows, w_rows, chunk_buf, own, partials, arrived, gathered, results, returned, count_ref, counts,
+    x_rows, w_rows, chunk_buf, own, partials, arrived, gathered, results, far_results, returned, far_returned, count_ref, counts,
     chunk_sem, count_send, count_recv, chan_send, chan_recv, beam_send, beam_recv, back_send, back_recv,
+    far_send, far_recv,
 ):
     groups, stations = lax.axis_size("chan"), lax.axis_size("station")
     mine, me = lax.axis_index("chan"), lax.axis_index("station")
@@ -72,11 +75,20 @@
             beam_send, beam_recv.at[i], (target(q * GROUP + u), mine),
         )
 
+    half = stations // 2
+    near_first = me // half * half
+    far_first = half - near_first
+
     def back_copy(i, k):
-        there = target(k)
-        return remote(
-            results.at[i, there], returned.at[i * stations + me],
-            back_send, back_recv, (there, mine),
+        there = near_first + lax.rem(me + 1 + k, half)
+        return remote(
+            results.at[i, there], returned.at[i * stations + me], back_send, back_recv, (there, mine)
+        )
+
+    def far_copy(i, k):
+        return remote(
+            far_results.at[i, k], far_returned.at[i, lax.rem(me, half)], far_send, far_recv,
+            (far_first + k, mine),
         )
 
     def all_of(ref, send, recv):
@@ -248,45 +260,53 @@
                     row = (part * beam_tiles + tile) * wide + piece
                     results[i, :, row, :] = total[:, piece * LANES : (piece + 1) * LANES]
 
-        @pl.loop(0, stations - 1)
+        far_results[i] = results[i, pl.ds(far_first, half)].astype(jnp.bfloat16)
+
+        @pl.loop(0, half)
+        def _(k):
+            far_copy(i, k).start()
+
+        @pl.loop(0, half - 1)
         def _(k):
             back_copy(i, k).start()
 
         returned[i * stations + me] = results[i, me]
 
-    peers(0, 0)
+    phases = halves * share
+    ahead, behind = min(AHEAD, share), min(BEHIND, share)
+    each = pl.cdiv(x_chunks, share - ahead + 1)
+
+    for p in range(ahead):
+        peers(0, p)
     count = count_ref[...]
     for g in range(1, groups):
         count_copy(g).wait_recv()
         count = count + counts[g - 1]
     gain = lax.rsqrt(count)[0:1, :]
 
-    each = x_chunks // share
-    for h in range(halves):
-        @pl.loop(0, share)
-        def _(i):
-            own_sums(h, i)
-            if h + 1 < halves:
-                turn(h + 1, i * each, (i + 1) * each)
-
-            @pl.when(i + 1 < share)
-            def _():
-                peers(h, i + 1)
-
-            if h + 1 < halves:
-                @pl.when(i + 1 == share)
-                def _():
-                    peers(h + 1, 0)
-
-            forward(h, i, gain)
-            if h + 1 == halves:
-                @pl.when(i > 0)
-                def _():
-                    correlate(i - 1)
-
-    correlate(share - 1)
-
-    all_of(returned.at[pl.ds(0, share * (stations - 1))], back_send, back_recv).wait_recv()
+    @pl.loop(0, phases)
+    def _(p):
+        turn(1, jnp.minimum(p * each, x_chunks * (halves - 1)), jnp.minimum((p + 1) * each, x_chunks * (halves - 1)))
+
+        @pl.when(p + ahead < phases)
+        def _():
+            peers((p + ahead) // share, lax.rem(p + ahead, share))
+
+        own_sums(p // share, lax.rem(p, share))
+        forward(p // share, lax.rem(p, share), gain)
+
+        @pl.when(p >= phases - share + behind)
+        def _():
+            correlate(p - (phases - share + behind))
+
+    @pl.loop(share - behind, share)
+    def _(i):
+        correlate(i)
+
+    all_of(returned.at[pl.ds(0, share * (half - 1))], back_send, back_recv).wait_recv()
+    all_of(far_returned, far_send, far_recv).wait_recv()
+    for i in range(share):
+        returned[pl.ds(i * stations + far_first, half)] = far_returned[i].astype(jnp.float32)
 
     per_row = LANES // TILE_BEAMS
     for part in range(2):
@@ -303,7 +323,8 @@
         count_copy(g).wait_send()
     all_of(partials, chan_send, chan_recv.at[0, 0, 0, 0]).wait_send()
     all_of(gathered.at[:, :, others], beam_send, beam_recv.at[0]).wait_send()
-    all_of(results.at[:, others], back_send, back_recv).wait_send()
+    all_of(results.at[:, pl.ds(0, half - 1)], back_send, back_recv).wait_send()
+    all_of(far_results, far_send, far_recv).wait_send()
 
 
 def on_device(samples, weights, antenna_flags, subband_table):
@@ -336,7 +357,9 @@
             pltpu.VMEM((groups - 1, halves, share, quarters, GROUP, beams, LANES), jnp.bfloat16),
             pltpu.VMEM((halves, share, stations, beams, LANES), jnp.bfloat16),
             pltpu.VMEM((share, stations, rows, LANES), jnp.float32),
+            pltpu.VMEM((share, stations // 2, rows, LANES), jnp.bfloat16),
             pltpu.VMEM((kept, rows, LANES), jnp.float32),
+            pltpu.VMEM((share, stations // 2, rows, LANES), jnp.bfloat16),
             pltpu.VMEM((8, LANES), jnp.float32),
             pltpu.VMEM((groups - 1, 8, LANES), jnp.float32),
             dma((CHUNKS_IN_FLIGHT,)),
@@ -346,6 +369,8 @@
             dma((groups - 1, halves, share, quarters)),
             dma,
             dma((share,)),
+            dma,
+            dma,
             dma,
             dma,
         ],

time: 88.4 us -> 77.9 us (0.88)
  Pallas kernels: 86.3 us -> 75.9 us
    pallas_call x1, Pallas kernels: 86.3 us -> 75.9 us  [on_device(): pl.pallas_call(kernel, out_shape=jax.ShapeDtypeStruct((2, beams, stations...]
where the time goes in v3:
time: 77.9 us; the launch traced here: 77.8 us
  Pallas kernels  75.9 us (97%)
  local copies, waits for them, and re-layouts  1.87 us (2%)
    pallas_call x1, Pallas kernels, on_device(): pl.pallas_call(kernel, out_shape=jax.ShapeDtypeStruct((2, beams, stations...  75.9 us
    unnamed x1, local copies, waits for them, and re-layouts  1.87 us

profile of v3, /device:TPU:0, one launch (start us, length us, event | category | flops | bytes accessed | tf_op | source)
XLA Modules:
  0.0 77.8 jit_solution(14836957032926101492)
XLA Ops:
  0.0 75.9 %shard_map.46 = f32[2,32,16,128]{3,2,1,0:T(8,128)} custom-call(s32[256]{0:T(256)} %table_ref.1, s32[1,128]{1,0:T(1,128)} %flags_ref.1, f32[2,1,128,128,256]{4,3,2,1,0:T(8,128)} %x_hbm.1, f32[2,1,64,64,256]{4,3,2,1,0:T(8,128)} %bitcast.6), custom_call_target="tpu_custom_call" | custom-call | tf_op jit(solution)/shard_map/pallas_call | solution.py:341
  75.9 1.9 %copy.7 = f32[128,2,1,32,16]{0,4,3,2,1:T(8,128)} copy(f32[128,2,1,32,16]{0,4,3,2,1:T(8,128)} %bitcast.7) | data formatting | bytes 1048576

commit v4 on v3

--- a/solution.py
+++ b/solution.py
@@ -243,6 +243,11 @@
     beam_tiles = beams // TILE_BEAMS
     result_rows = 2 * beam_tiles * wide
 
+    def spare(shape, station):
+        row, place = lax.broadcasted_iota(jnp.int32, shape, 1), lax.broadcasted_iota(jnp.int32, shape, 2)
+        other = lax.rem(row, wide) * (LANES // TILE_BEAMS) + place // TILE_BEAMS
+        return (row >= result_rows // 2) & (other == station)
+
     def correlate(i):
         all_of(gathered.at[:, i, others], beam_send, beam_recv.at[i]).wait_recv()
         for tile in range(beam_tiles):
@@ -260,7 +265,12 @@
                     row = (part * beam_tiles + tile) * wide + piece
                     results[i, :, row, :] = total[:, piece * LANES : (piece + 1) * LANES]
 
-        far_results[i] = results[i, pl.ds(far_first, half)].astype(jnp.bfloat16)
+        value = results[i, pl.ds(far_first, half)]
+        low = value - value.astype(jnp.bfloat16).astype(jnp.float32)
+        station = far_first + lax.broadcasted_iota(jnp.int32, value.shape, 0)
+        far_results[i] = jnp.where(
+            spare(value.shape, station), pltpu.roll(low, result_rows // 2, axis=1), value
+        ).astype(jnp.bfloat16)
 
         @pl.loop(0, half)
         def _(k):
@@ -306,7 +316,10 @@
     all_of(returned.at[pl.ds(0, share * (half - 1))], back_send, back_recv).wait_recv()
     all_of(far_returned, far_send, far_recv).wait_recv()
     for i in range(share):
-        returned[pl.ds(i * stations + far_first, half)] = far_returned[i].astype(jnp.float32)
+        value = far_returned[i].astype(jnp.float32)
+        extra = spare(value.shape, me)
+        low = pltpu.roll(jnp.where(extra, value, 0.0), result_rows // 2, axis=1)
+        returned[pl.ds(i * stations + far_first, half)] = jnp.where(extra, 0.0, value + low)
 
     per_row = LANES // TILE_BEAMS
     for part in range(2):

time: 77.9 us -> 77.9 us (level)
  no operation moved by 1% of the time
where the time goes in v4:
time: 77.9 us; the launch traced here: 77.7 us
  Pallas kernels  75.8 us (97%)
  local copies, waits for them, and re-layouts  1.87 us (2%)
    pallas_call x1, Pallas kernels, on_device(): pl.pallas_call(kernel, out_shape=jax.ShapeDtypeStruct((2, beams, stations...  75.8 us
    unnamed x1, local copies, waits for them, and re-layouts  1.87 us

profile of v4, /device:TPU:0, one launch (start us, length us, event | category | flops | bytes accessed | tf_op | source)
XLA Modules:
  0.0 77.7 jit_solution(738471287961552147)
XLA Ops:
  0.0 75.8 %shard_map.46 = f32[2,32,16,128]{3,2,1,0:T(8,128)} custom-call(s32[256]{0:T(256)} %table_ref.1, s32[1,128]{1,0:T(1,128)} %flags_ref.1, f32[2,1,128,128,256]{4,3,2,1,0:T(8,128)} %x_hbm.1, f32[2,1,64,64,256]{4,3,2,1,0:T(8,128)} %bitcast.6), custom_call_target="tpu_custom_call" | custom-call | tf_op jit(solution)/shard_map/pallas_call | solution.py:354
  75.8 1.9 %copy.7 = f32[128,2,1,32,16]{0,4,3,2,1:T(8,128)} copy(f32[128,2,1,32,16]{0,4,3,2,1:T(8,128)} %bitcast.7) | data formatting | bytes 1048576

commit v5 on v4

--- a/solution.py
+++ b/solution.py
@@ -10,8 +10,9 @@
 LANES = 128
 SLAB = 64
 SLABS_PER_CHUNK = 8
-CHUNKS_IN_FLIGHT = 8
+CHUNKS_IN_FLIGHT = 5
 GROUP = 8
+UNROLL = 16
 TILE_BEAMS = 16
 AHEAD = 3
 BEHIND = 3
@@ -24,9 +25,9 @@
 
 
 def kernel(
-    table_ref, flags_ref, x_hbm, w_hbm, out_ref,
-    x_rows, w_rows, chunk_buf, own, partials, arrived, gathered, results, far_results, returned, far_returned, count_ref, counts,
-    chunk_sem, count_send, count_recv, chan_send, chan_recv, beam_send, beam_recv, back_send, back_recv,
+    table_hbm, flags_hbm, x_hbm, w_hbm, out_ref,
+    table_ref, flags_ref, rows, chunk_buf, own, partials, arrived, gathered, results, far_results, returned, far_returned, count_ref, counts,
+    small_sem, chunk_sem, count_send, count_recv, chan_send, chan_recv, beam_send, beam_recv, back_send, back_recv,
     far_send, far_recv,
 ):
     groups, stations = lax.axis_size("chan"), lax.axis_size("station")
@@ -38,15 +39,14 @@
     kept = subbands // groups
     blocks = subbands // LANES
     tall = min(antennas, SLAB)
-    x_stride = x_rows.shape[2]
-    w_stride = w_rows.shape[1]
+    stride = rows.shape[1]
+    w_first = halves * antennas
     w_chunks = w_hbm.shape[2] // SLABS_PER_CHUNK
     x_chunks = antennas // SLABS_PER_CHUNK
     chunks = w_chunks + halves * x_chunks
     beams_per_chunk = SLABS_PER_CHUNK * SLAB // antennas
     parts_of_phase = stations // GROUP
-    x_lines = x_rows.reshape(halves, subbands * x_stride, LANES)
-    w_lines = w_rows.reshape(subbands * w_stride, LANES)
+    lines = rows.reshape(subbands * stride, LANES)
 
     def target(k):
         return lax.rem(me + stations // 2 + ((k + 1) // 2) * (1 - 2 * lax.rem(k, 2)), stations)
@@ -82,7 +82,7 @@
     def back_copy(i, k):
         there = near_first + lax.rem(me + 1 + k, half)
         return remote(
-            results.at[i, there], returned.at[i * stations + me], back_send, back_recv, (there, mine)
+            results.at[i, there], returned.at[i, lax.rem(me, half)], back_send, back_recv, (there, mine)
         )
 
     def far_copy(i, k):
@@ -121,6 +121,10 @@
         def _():
             x_copy(n - w_chunks, slot_of(n)).start()
 
+    flags_copy = pltpu.make_async_copy(flags_hbm, flags_ref, small_sem.at[0])
+    table_copy = pltpu.make_async_copy(table_hbm, table_ref, small_sem.at[1])
+    flags_copy.start()
+    table_copy.start()
     for n in range(min(CHUNKS_IN_FLIGHT, chunks)):
         if n < w_chunks:
             w_copy(n, n % CHUNKS_IN_FLIGHT).start()
@@ -137,6 +141,7 @@
     def _(k):
         pl.semaphore_signal(barrier, inc=1, device_id=(target(k), mine), device_id_type=pl.DeviceIdType.MESH)
 
+    flags_copy.wait()
     usable = flags_ref[...].astype(jnp.float32)
     count_ref[...] = jnp.broadcast_to(jnp.sum(usable, axis=1, keepdims=True), count_ref.shape)
     if antennas < LANES:
@@ -156,8 +161,8 @@
                     ]
                     if antennas < LANES:
                         tiles.append(jnp.zeros((LANES - antennas, LANES), jnp.float32))
-                    row = block * LANES * w_stride + part * beams + n * beams_per_chunk + b
-                    w_lines[pl.ds(row, LANES, stride=w_stride), :] = jnp.concatenate(tiles, axis=0).T * usable
+                    row = block * LANES * stride + w_first + part * beams + n * beams_per_chunk + b
+                    lines[pl.ds(row, LANES, stride=stride), :] = jnp.concatenate(tiles, axis=0).T * usable
         start_chunk(n + CHUNKS_IN_FLIGHT)
 
     def turn(h, first, last):
@@ -170,12 +175,13 @@
                 for block in range(blocks):
                     lanes = pl.ds(block * LANES, LANES)
                     tile = jnp.concatenate([chunk_buf[slot, part, a, :, lanes] for part in range(2)], axis=0)
-                    row = block * LANES * x_stride + m * SLABS_PER_CHUNK + a
-                    x_lines[h, pl.ds(row, LANES, stride=x_stride), :] = tile.T
+                    row = block * LANES * stride + h * antennas + m * SLABS_PER_CHUNK + a
+                    lines[pl.ds(row, LANES, stride=stride), :] = tile.T
             start_chunk(n + CHUNKS_IN_FLIGHT)
 
     turn(0, 0, x_chunks)
 
+    table_copy.wait()
     pl.semaphore_wait(barrier, groups - 1 + stations - 1)
     for g in range(1, groups):
         count_copy(g).start()
@@ -185,8 +191,8 @@
 
     def partial(h, slot):
         f = table_ref[slot]
-        x = x_rows[h, f, :antennas, :]
-        w = w_rows[f, : 2 * beams, :antennas]
+        x = rows[f, pl.ds(pl.multiple_of(h * antennas, 8), antennas), :]
+        w = rows[f, w_first : w_first + 2 * beams, :antennas]
         x_pair = jnp.concatenate(split(x), axis=0)
         w_high, w_low = split(w)
         grid = jnp.dot(
@@ -198,20 +204,24 @@
         for g in range(1, groups):
             first = lax.rem(mine + g, groups) * kept + i * stations
 
-            @pl.loop(0, parts_of_phase)
-            def _(q):
-                for u in range(GROUP):
-                    total = partial(h, first + target(q * GROUP + u))
-                    partials[g - 1, h, i, q, u] = total.astype(jnp.bfloat16)
-                chan_copy(g, h, i, q).start()
+            @pl.loop(0, stations // UNROLL)
+            def _(v):
+                for w in range(UNROLL // GROUP):
+                    q = v * (UNROLL // GROUP) + w
+                    for u in range(GROUP):
+                        total = partial(h, first + target(q * GROUP + u))
+                        partials[g - 1, h, i, q, u] = total.astype(jnp.bfloat16)
+                    chan_copy(g, h, i, q).start()
 
     def own_sums(h, i):
         first = mine * kept + i * stations
 
-        @pl.loop(0, parts_of_phase)
-        def _(q):
-            for u in range(GROUP):
-                own[q, u] = partial(h, first + target(q * GROUP + u))
+        @pl.loop(0, stations // UNROLL)
+        def _(v):
+            for w in range(UNROLL // GROUP):
+                q = v * (UNROLL // GROUP) + w
+                for u in range(GROUP):
+                    own[q, u] = partial(h, first + target(q * GROUP + u))
 
     def forward(h, i, gain):
         def piece(q, last):
@@ -280,7 +290,7 @@
         def _(k):
             back_copy(i, k).start()
 
-        returned[i * stations + me] = results[i, me]
+        returned[i, lax.rem(me, half)] = results[i, me]
 
     phases = halves * share
     ahead, behind = min(AHEAD, share), min(BEHIND, share)
@@ -296,15 +306,15 @@
 
     @pl.loop(0, phases)
     def _(p):
+        own_sums(p // share, lax.rem(p, share))
+        forward(p // share, lax.rem(p, share), gain)
+
         turn(1, jnp.minimum(p * each, x_chunks * (halves - 1)), jnp.minimum((p + 1) * each, x_chunks * (halves - 1)))
 
         @pl.when(p + ahead < phases)
         def _():
             peers((p + ahead) // share, lax.rem(p + ahead, share))
 
-        own_sums(p // share, lax.rem(p, share))
-        forward(p // share, lax.rem(p, share), gain)
-
         @pl.when(p >= phases - share + behind)
         def _():
             correlate(p - (phases - share + behind))
@@ -313,20 +323,22 @@
     def _(i):
         correlate(i)
 
-    all_of(returned.at[pl.ds(0, share * (half - 1))], back_send, back_recv).wait_recv()
+    all_of(returned.at[:, pl.ds(0, half - 1)], back_send, back_recv).wait_recv()
+    all_of(results.at[:, pl.ds(0, half - 1)], back_send, back_recv).wait_send()
     all_of(far_returned, far_send, far_recv).wait_recv()
     for i in range(share):
         value = far_returned[i].astype(jnp.float32)
         extra = spare(value.shape, me)
         low = pltpu.roll(jnp.where(extra, value, 0.0), result_rows // 2, axis=1)
-        returned[pl.ds(i * stations + far_first, half)] = jnp.where(extra, 0.0, value + low)
+        results[i, pl.ds(far_first, half)] = jnp.where(extra, 0.0, value + low)
+        results[i, pl.ds(near_first, half)] = returned[i]
 
     per_row = LANES // TILE_BEAMS
     for part in range(2):
         for tile in range(beam_tiles):
             for piece in range(wide):
                 row = (part * beam_tiles + tile) * wide + piece
-                turned = returned[:, row, :].T
+                turned = results[:, :, row, :].reshape(kept, LANES).T
                 for r in range(per_row):
                     out_ref[part, pl.ds(tile * TILE_BEAMS, TILE_BEAMS), piece * per_row + r, :] = turned[
                         r * TILE_BEAMS : (r + 1) * TILE_BEAMS
@@ -336,7 +348,6 @@
         count_copy(g).wait_send()
     all_of(partials, chan_send, chan_recv.at[0, 0, 0, 0]).wait_send()
     all_of(gathered.at[:, :, others], beam_send, beam_recv.at[0]).wait_send()
-    all_of(results.at[:, pl.ds(0, half - 1)], back_send, back_recv).wait_send()
     all_of(far_results, far_send, far_recv).wait_send()
 
 
@@ -348,33 +359,35 @@
     share = kept // stations
     halves = times // SLAB
     quarters = stations // GROUP
-    rows = 2 * (beams // TILE_BEAMS) * (stations * TILE_BEAMS // LANES)
+    result_rows = 2 * (beams // TILE_BEAMS) * (stations * TILE_BEAMS // LANES)
     slabs = weights.reshape(2, 1, beams * antennas // SLAB, SLAB, subbands)
     dma = pltpu.SemaphoreType.DMA
     out = pl.pallas_call(
         kernel,
         out_shape=jax.ShapeDtypeStruct((2, beams, stations, kept), jnp.float32),
         in_specs=[
-            pl.BlockSpec(memory_space=pltpu.SMEM),
-            pl.BlockSpec(memory_space=pltpu.VMEM),
+            pl.BlockSpec(memory_space=pltpu.HBM),
+            pl.BlockSpec(memory_space=pltpu.HBM),
             pl.BlockSpec(memory_space=pl.ANY),
             pl.BlockSpec(memory_space=pl.ANY),
         ],
         out_specs=pl.BlockSpec(memory_space=pltpu.VMEM),
         scratch_shapes=[
-            pltpu.VMEM((halves, subbands, antennas + 8, LANES), jnp.float32),
-            pltpu.VMEM((subbands, 2 * beams + 8, LANES), jnp.float32),
+            pltpu.SMEM((subbands,), jnp.int32),
+            pltpu.VMEM((1, antennas), jnp.int32),
+            pltpu.VMEM((subbands, halves * antennas + 2 * beams + 8, LANES), jnp.float32),
             pltpu.VMEM((CHUNKS_IN_FLIGHT, 2, SLABS_PER_CHUNK, SLAB, subbands), jnp.float32),
             pltpu.VMEM((quarters, GROUP, beams, LANES), jnp.float32),
             pltpu.VMEM((groups - 1, halves, share, quarters, GROUP, beams, LANES), jnp.bfloat16),
             pltpu.VMEM((groups - 1, halves, share, quarters, GROUP, beams, LANES), jnp.bfloat16),
             pltpu.VMEM((halves, share, stations, beams, LANES), jnp.bfloat16),
-            pltpu.VMEM((share, stations, rows, LANES), jnp.float32),
-            pltpu.VMEM((share, stations // 2, rows, LANES), jnp.bfloat16),
-            pltpu.VMEM((kept, rows, LANES), jnp.float32),
-            pltpu.VMEM((share, stations // 2, rows, LANES), jnp.bfloat16),
+            pltpu.VMEM((share, stations, result_rows, LANES), jnp.float32),
+            pltpu.VMEM((share, stations // 2, result_rows, LANES), jnp.bfloat16),
+            pltpu.VMEM((share, stations // 2, result_rows, LANES), jnp.float32),
+            pltpu.VMEM((share, stations // 2, result_rows, LANES), jnp.bfloat16),
             pltpu.VMEM((8, LANES), jnp.float32),
             pltpu.VMEM((groups - 1, 8, LANES), jnp.float32),
+            dma((2,)),
             dma((CHUNKS_IN_FLIGHT,)),
             dma((groups - 1,)),
             dma((groups - 1,)),
@@ -388,7 +401,7 @@
             dma,
         ],
         compiler_params=pltpu.CompilerParams(
-            collective_id=0, has_side_effects=True, vmem_limit_bytes=67043328
+            collective_id=0, has_side_effects=True, vmem_limit_bytes=56000000
         ),
     )(subband_table, antenna_flags, samples, slabs)
     return out.transpose(3, 0, 1, 2)[:, :, None]

time: 77.9 us -> 76.5 us (0.982)
  Pallas kernels: 75.8 us -> 74.2 us
    pallas_call x1, Pallas kernels: 75.8 us -> 74.2 us  [on_device(): pl.pallas_call(kernel, out_shape=jax.ShapeDtypeStruct((2, beams, stations...]
    unnamed x1 -> x5, local copies, waits for them, and re-layouts: 1.87 us -> 2.13 us
where the time goes in v5:
time: 76.5 us; the launch traced here: 76.3 us
  Pallas kernels  74.2 us (97%)
  local copies, waits for them, and re-layouts  2.13 us (3%)
    pallas_call x1, Pallas kernels, on_device(): pl.pallas_call(kernel, out_shape=jax.ShapeDtypeStruct((2, beams, stations...  74.2 us
    unnamed x5, local copies, waits for them, and re-layouts  2.13 us

profile of v5, /device:TPU:0, one launch (start us, length us, event | category | flops | bytes accessed | tf_op | source)
XLA Modules:
  0.0 76.3 jit_solution(14627777265354074353)
XLA Ops:
  0.0 0.0 copy-start
  0.0 0.7 copy-done
  0.7 0.0 copy-start.1
  0.7 0.7 copy-done.1
  1.3 74.2 %shard_map.46 = f32[2,32,16,128]{3,2,1,0:T(8,128)S(1)} custom-call(s32[256]{0:T(256)S(1)} %copy-done, s32[1,128]{1,0:T(1,128)S(1)} %copy-done.1, f32[2,1,128,128,256]{4,3,2,1,0:T(8,128)} %x_hbm.1, f32[2,1,64,64,256]{4,3,2,1,0:T(8,128)} %bitcast.7), custom_call_target="tpu_custom_call" | custom-call | tf_op jit(solution)/shard_map/pallas_call | solution.py:365
  75.6 0.8 %copy.7 = f32[128,2,1,32,16]{0,4,3,2,1:T(8,128)} copy(f32[128,2,1,32,16]{0,4,3,2,1:T(8,128)S(1)} %bitcast.6) | data formatting | bytes 1048576
Async XLA Ops:
  0.0 0.7 copy-start
  0.7 0.7 copy-start.1

commit v6 on v5

--- a/solution.py
+++ b/solution.py
@@ -49,7 +49,11 @@
     lines = rows.reshape(subbands * stride, LANES)
 
     def target(k):
-        return lax.rem(me + stations // 2 + ((k + 1) // 2) * (1 - 2 * lax.rem(k, 2)), stations)
+        middle = stations // 2
+        side = me // middle
+        across = (1 - side) * middle + lax.rem(me + k, middle)
+        beside = side * middle + lax.rem(me + 1 + k, middle)
+        return jnp.where(k < middle, across, beside)
 
     def remote(src, dst, send, recv, device):
         return pltpu.make_async_remote_copy(

time: 76.5 us -> 76.6 us (level)
  no operation moved by 1% of the time
where the time goes in v6:
time: 76.6 us; the launch traced here: 76.4 us
  Pallas kernels  74.3 us (97%)
  local copies, waits for them, and re-layouts  2.13 us (3%)
    pallas_call x1, Pallas kernels, on_device(): pl.pallas_call(kernel, out_shape=jax.ShapeDtypeStruct((2, beams, stations...  74.3 us
    unnamed x5, local copies, waits for them, and re-layouts  2.13 us

profile of v6, /device:TPU:0, one launch (start us, length us, event | category | flops | bytes accessed | tf_op | source)
XLA Modules:
  0.0 76.4 jit_solution(14704917556137381541)
XLA Ops:
  0.0 0.0 copy-start
  0.0 0.7 copy-done
  0.7 0.0 copy-start.1
  0.7 0.7 copy-done.1
  1.3 74.3 %shard_map.46 = f32[2,32,16,128]{3,2,1,0:T(8,128)S(1)} custom-call(s32[256]{0:T(256)S(1)} %copy-done, s32[1,128]{1,0:T(1,128)S(1)} %copy-done.1, f32[2,1,128,128,256]{4,3,2,1,0:T(8,128)} %x_hbm.1, f32[2,1,64,64,256]{4,3,2,1,0:T(8,128)} %bitcast.7), custom_call_target="tpu_custom_call" | custom-call | tf_op jit(solution)/shard_map/pallas_call | solution.py:369
  75.6 0.8 %copy.7 = f32[128,2,1,32,16]{0,4,3,2,1:T(8,128)} copy(f32[128,2,1,32,16]{0,4,3,2,1:T(8,128)S(1)} %bitcast.6) | data formatting | bytes 1048576
Async XLA Ops:
  0.0 0.7 copy-start
  0.7 0.7 copy-start.1
